TPU v7x, 32 devices: a whole 2x2x4 slice. The times are simulated.
32 devices in a mesh: gx: 4 (over x, core), gy: 8 (over z, y).
Axes of the slice: x: 2, y: 2, z: 4, core: 2. Of those that a mesh axis runs over, the one named last changes fastest.
Arguments:
- mask_feats: bfloat16 [64, 8, 14, 14, 256], P(('gx', 'gy')), may hold values from -6 to 6
- mask_cot: bfloat16 [64, 8, 14, 14, 256], P(('gx', 'gy')), may hold values from -6 to 6
- roi_counts: int32 [64], P(('gx', 'gy')), may hold values from 1 to 8, as said below
- rpn_feats: bfloat16 [64, 48, 32, 256], P(('gx', 'gy')), may hold values from -6 to 6
- rpn_cot: bfloat16 [64, 48, 32, 256], P(('gx', 'gy')), may hold values from -360 to 360
- anchor_counts: int32 [64], P(('gx', 'gy')), may hold values from 32 to 223
- mask_weight: float32 [2304, 256], replicated, may hold values from -0.125 to 0.125
- rpn_weight: float32 [2304, 256], replicated, may hold values from -0.125 to 0.125
- mask_moment: float32 [2304, 256], replicated, may hold values from -6 to 6
- rpn_moment: float32 [2304, 256], replicated, may hold values from -6 to 6
Outputs:
- new_mask_weight: float32 [2304, 256], replicated
- new_rpn_weight: float32 [2304, 256], replicated
- new_mask_moment: float32 [2304, 256], replicated
- new_rpn_moment: float32 [2304, 256], replicated
Inputs may be any that keep to these rules, and one draw needn't show every extreme that they name: `roi_counts`: every image has at least one positive ROI; some image has all 8 slots positive.
All inputs are finite; a program needn't handle non-finite values.
Results may differ from a plain program's by a relative error of at most 0.0003.
Values sent between devices are 32-bit elements; how exact they have to be, the bound alone decides.
A program may use at most 128 MiB of HBM per device.

v0:
```python
import jax
import jax.numpy as jnp
from jax import lax
from jax.sharding import PartitionSpec as P


def weight_grad(feats, cotan):
    grid_rows = feats.shape[1]
    grid_cols = feats.shape[2]
    chans = feats.shape[3]
    padded = jnp.pad(feats, ((0, 0), (1, 1), (1, 1), (0, 0)))
    flat_cot = cotan.reshape(-1, chans)
    blocks = []
    for row_tap in range(3):
        for col_tap in range(3):
            window = padded[
                :, row_tap : row_tap + grid_rows, col_tap : col_tap + grid_cols, :
            ].reshape(-1, chans)
            blocks.append(
                lax.dot_general(
                    window, flat_cot, (((0,), (0,)), ((), ())), preferred_element_type=jnp.float32
                )
            )
    return jnp.concatenate(blocks, axis=0)


def step_update(weight, moment, grad):
    fresh_moment = 0.9 * moment + grad
    return (weight - 0.02 * fresh_moment, fresh_moment)


def on_device(
    mask_feats,
    mask_cot,
    roi_counts,
    rpn_feats,
    rpn_cot,
    anchor_counts,
    mask_weight,
    rpn_weight,
    mask_moment,
    rpn_moment,
):
    slot_count = mask_feats.shape[1]
    side = mask_feats.shape[2]
    chans = mask_feats.shape[4]
    slots = jnp.arange(slot_count, dtype=jnp.int32)
    valid_slots = (slots[None, :] < roi_counts[:, None]).astype(jnp.bfloat16)
    masked = mask_cot * valid_slots[:, :, None, None, None]
    mask_local = weight_grad(
        mask_feats.reshape(-1, side, side, chans), masked.reshape(-1, side, side, chans)
    )
    rpn_local = weight_grad(rpn_feats, rpn_cot)
    local_counts = jnp.stack([jnp.sum(roi_counts), jnp.sum(anchor_counts)]).astype(jnp.float32)
    mask_sum, rpn_sum, totals = lax.psum((mask_local, rpn_local, local_counts), ("gx", "gy"))
    mask_grad = mask_sum / totals[0]
    rpn_grad = rpn_sum / totals[1]
    new_mask_weight, new_mask_moment = step_update(mask_weight, mask_moment, mask_grad)
    new_rpn_weight, new_rpn_moment = step_update(rpn_weight, rpn_moment, rpn_grad)
    return (new_mask_weight, new_rpn_weight, new_mask_moment, new_rpn_moment)


def solution(mesh):
    placed = (
        P(("gx", "gy"), None, None, None, None),
        P(("gx", "gy"), None, None, None, None),
        P(("gx", "gy")),
        P(("gx", "gy"), None, None, None),
        P(("gx", "gy"), None, None, None),
        P(("gx", "gy")),
        P(),
        P(),
        P(),
        P(),
    )
    return jax.shard_map(
        on_device, mesh=mesh, in_specs=placed, out_specs=(P(), P(), P(), P()), check_vma=False
    )
```

profile of v0, /device:TPU:0, one launch (start us, length us, event | category | flops | bytes accessed | tf_op | source)
XLA Modules:
  0.0 258.9 jit_solution(18293968853926520437)
XLA Ops:
  7.2 0.0 copy-start
  7.2 0.0 all-reduce.5.cloned.1.call-start
  7.2 0.8 compare_convert_fusion
  8.1 1.6 broadcast_multiply_fusion
  9.7 1.6 copy.29
  11.3 3.7 %reshape_reshape.3 = bf16[3136,256]{1,0:T(8,128)(2,1)} reshape(bf16[2,8,14,14,256]{4,3,2,1,0:T(8,128)(2,1)} %copy.29) | data formatting | bytes 3211264 | tf_op jit(solution)/shard_map/reshape;reshape | solution.py:12
  15.0 1.6 copy.81
  16.5 4.3 %pad_slice_fusion = (bf16[16,14,14,256]{3,0,2,1:T(8,128)(2,1)}, bf16[16,14,14,256]{3,0,2,1:T(8,128)(2,1)}, bf16[16,14,14,256]{3,0,2,1:T(8,128)(2,1)}, bf16[16,14...) fusion(bf16[16,14,14,256]{3,0,2,1:T(8,128)(2,1)S(1)} %bitcast.89), kind=kLoop, calls=%fused_computation.4 | loop fusion | bytes 14450688 | tf_op jit(solution)/shard_map/slice | solution.py:16
  20.8 1.8 copy.28
  22.7 3.6 %reshape.70 = bf16[3136,256]{1,0:T(8,128)(2,1)} reshape(bf16[16,14,14,256]{3,2,1,0:T(8,128)(2,1)} %copy.28) | data formatting | bytes 3211264 | tf_op jit(solution)/shard_map/reshape | solution.py:18
  26.3 3.3 %copy.30 = bf16[16,14,14,256]{3,2,1,0:T(8,128)(2,1)} copy(bf16[16,14,14,256]{3,0,2,1:T(8,128)(2,1)} %get-tuple-element.11) | data formatting | bytes 3211264 | tf_op jit(solution)/shard_map/slice | solution.py:16
  29.6 3.6 %reshape.71 = bf16[3136,256]{1,0:T(8,128)(2,1)} reshape(bf16[16,14,14,256]{3,2,1,0:T(8,128)(2,1)} %copy.30) | data formatting | bytes 3211264 | tf_op jit(solution)/shard_map/reshape | solution.py:18
  33.2 3.3 %copy.31 = bf16[16,14,14,256]{3,2,1,0:T(8,128)(2,1)} copy(bf16[16,14,14,256]{3,0,2,1:T(8,128)(2,1)} %get-tuple-element.12) | data formatting | bytes 3211264 | tf_op jit(solution)/shard_map/slice | solution.py:16
  36.5 3.6 %reshape.72 = bf16[3136,256]{1,0:T(8,128)(2,1)} reshape(bf16[16,14,14,256]{3,2,1,0:T(8,128)(2,1)} %copy.31) | data formatting | bytes 3211264 | tf_op jit(solution)/shard_map/reshape | solution.py:18
  40.1 3.3 %copy.32 = bf16[16,14,14,256]{3,2,1,0:T(8,128)(2,1)} copy(bf16[16,14,14,256]{3,0,2,1:T(8,128)(2,1)} %get-tuple-element.13) | data formatting | bytes 3211264 | tf_op jit(solution)/shard_map/slice | solution.py:16
  43.3 3.6 %reshape.73 = bf16[3136,256]{1,0:T(8,128)(2,1)} reshape(bf16[16,14,14,256]{3,2,1,0:T(8,128)(2,1)} %copy.32) | data formatting | bytes 3211264 | tf_op jit(solution)/shard_map/reshape | solution.py:18
  47.0 3.4 %convolution_dynamic-update-slice_fusion.7 = f32[2304,256]{1,0:T(8,128)} fusion(bf16[3136,256]{1,0:T(8,128)(2,1)} %reshape.70, bf16[3136,256]{1,0:T(8,128)(2,1)} %reshape_reshape.3), kind=kOutput, calls=%fused_computation.36 | convolution fusion | flops 411041792 | bytes 3473408 | tf_op jit(solution)/shard_map/dot_general | solution.py:20
  50.4 1.3 convolution_dynamic-update-slice_fusion.6
  51.7 0.1 copy-done.12
  51.8 1.3 convolution_dynamic-update-slice_fusion.5
  53.2 0.1 copy-done.13
  53.2 1.3 convolution_dynamic-update-slice_fusion.4
  54.6 0.1 copy-done.2
  54.7 1.5 fusion.25
  56.2 0.6 copy.35
  56.8 1.4 reshape.74
  58.2 2.0 copy.36
  60.2 1.4 reshape.75
  61.6 2.0 copy.37
  63.6 1.4 reshape.76
  65.0 2.0 copy.38
  67.1 1.4 reshape.77
  68.5 2.3 copy.39
  70.8 1.8 fusion.24
  72.6 2.1 fusion.22
  74.7 2.0 fusion.20
  76.7 0.0 copy-start.3
  76.7 1.3 fusion.18
  78.1 0.1 copy-done.3
  78.1 0.6 fusion.8
  78.8 1.3 fusion.16
  80.1 2.1 fusion.14
  82.2 2.3 fusion.12
  84.5 0.0 copy-start.7
  84.5 2.1 fusion.10
  86.6 0.0 copy-start.4
  86.6 0.0 copy-start.8
  86.6 1.3 convolution_dynamic-update-slice_fusion.3
  88.0 0.1 copy-done.4
  88.1 0.9 copy-done.8
  89.0 1.4 convolution_dynamic-update-slice_fusion.2
  90.3 0.1 copy-done.9
  90.4 1.4 convolution_dynamic-update-slice_fusion.1
  91.8 0.0 copy-done.10
  91.8 1.4 convolution_dynamic-update-slice_fusion
  93.2 0.0 all-reduce.5.cloned.1.call-update
  93.2 0.6 copy-done.14
  93.8 0.6 reduce_sum.18
  94.5 0.6 reduce_sum.19
  95.1 1.4 add_convert_fusion
  96.5 42.4 %psum.22 = f32[2]{0:T(128)S(1)} all-reduce(f32[2]{0:T(128)S(1)} %add_convert_fusion), channel_id=1, replica_groups=mesh['gx'=4,'gy'=8] {'gx','gy'}, use_global_device_ids=true, to_apply=%region_3.4 | all-reduce | flops 2 | bytes 16 | tf_op jit(solution)/shard_map/psum | solution.py:55
  138.9 0.7 fusion.42
  139.5 101.9 %all-reduce.5.cloned.1.call-done = (f32[2304,256]{1,0:T(8,128)}, f32[2304,256]{1,0:T(8,128)}) async-done(((f32[2304,256]{1,0:T(8,128)}, f32[2304,256]{1,0:T(8,128)}), (f32[2304,256]{1,0:T(8,128)}, f32[2304,256]{1,0:T(8,128)})) %all-reduce.5.cloned.1.call-update) | async-done | bytes 4718608 | tf_op jit(solution)/shard_map/psum | solution.py:55
  241.5 10.6 %multiply_subtract_fusion = (f32[2304,256]{1,0:T(8,128)}, f32[2304,256]{1,0:T(8,128)}, f32[2304,256]{1,0:T(8,128)}, f32[2304,256]{1,0:T(8,128)}) fusion(f32[2304,256]{1,0:T(8,128)} %param.17, f32[2304,256]{1,0:T(8,128)} %get-tuple-element.5, f32[]{:T(128)} %bitcast.25, f32[2304,256]{1,0:T(8,128)} %param.19, f32[2304,256]{1,0:T(8,128)} %param.16, ...), kind=kLoop, calls=%fused_computation | loop fusion | flops 5898240 | bytes 23592968 | tf_op jit(solution)/shard_map/sub | solution.py:29
  (18 shorter events, 0.0 us)
Async XLA Ops:
  7.2 63.6 %copy-start = (bf16[2,48,32,256]{3,2,1,0:T(8,128)(2,1)S(1)}, bf16[2,48,32,256]{3,2,1,0:T(8,128)(2,1)}, u32[]{:S(2)}) copy-start(bf16[2,48,32,256]{3,2,1,0:T(8,128)(2,1)} %param.14) | copy-start | bytes 4718596
  7.2 234.3 %all-reduce.5.cloned.1.call-start = ((), (), s32[]{:S(2)}) async-start(), calls=%async_computation | async-start | bytes 9437184 | tf_op jit(solution)/shard_map/psum | solution.py:55
  47.0 3.4 %copy-start.5 = (bf16[3136,256]{1,0:T(8,128)(2,1)S(1)}, bf16[3136,256]{1,0:T(8,128)(2,1)}, u32[]{:S(2)}) copy-start(bf16[3136,256]{1,0:T(8,128)(2,1)} %reshape_reshape.3) | copy-start | bytes 4816900
  47.0 3.4 %copy-start.11 = (bf16[3136,256]{1,0:T(8,128)(2,1)S(1)}, bf16[3136,256]{1,0:T(8,128)(2,1)}, u32[]{:S(2)}) copy-start(bf16[3136,256]{1,0:T(8,128)(2,1)} %reshape.71) | copy-start | bytes 4816900
  50.4 1.4 copy-start.12
  51.8 1.4 copy-start.13
  53.2 1.4 copy-start.2
  54.7 1.5 copy-start.1
  76.7 1.4 copy-start.3
  84.5 2.1 copy-start.6
  84.5 2.1 copy-start.7
  86.6 1.5 copy-start.4
  86.6 2.4 copy-start.8
  89.0 1.4 copy-start.9
  90.4 1.4 copy-start.10
  93.2 0.7 copy-start.14
  93.2 1.3 copy-start.15
Sparse Core Ops, SparseCore 0:
  93.3 148.0 all-reduce.4
where the time goes:
time: 260 us; the launch traced here: 259 us
  waiting for transfers between devices  102 us (39%)
  local copies, waits for them, and re-layouts  54.6 us (21%)
  blocking collectives  42.4 us (16%)
  matrix products  30 us (12%)
  other arithmetic  15.6 us (6%)
  between operations  14.2 us (5%)
    psum x1, waiting for transfers between devices, on_device(): lax.psum((mask_local, rpn_local, local_counts), ('gx', 'gy'))  102 us
    psum x1, blocking collectives, on_device(): lax.psum((mask_local, rpn_local, local_counts), ('gx', 'gy'))  42.4 us
    dot_general x18, matrix products, weight_grad(): lax.dot_general(window, flat_cot, (((0,), (0,)), ((), ())), preferred_ele...  30 us
    slice x9, local copies, waits for them, and re-layouts, weight_grad(): padded[:, row_tap:row_tap + grid_rows, col_tap:col_tap + grid_cols, :]  22.6 us
    reshape x8, local copies, waits for them, and re-layouts, weight_grad(): window = padded[:, row_tap:row_tap + grid_rows, col_tap:col_tap + grid_co...  20.2 us
    sub x1, other arithmetic, step_update(): return (weight - 0.02 * fresh_moment, fresh_moment)  10.6 us
    unnamed x34, local copies, waits for them, and re-layouts  5.92 us
  transfers between devices with their start and end apart: 1, of which 1 were waited for; matrix products, arithmetic and copies ran while one was open for 1% of the time, Pallas kernels for 0%

commit v1 on v0

--- a/solution.py
+++ b/solution.py
@@ -2,6 +2,11 @@
 import jax.numpy as jnp
 from jax import lax
 from jax.sharding import PartitionSpec as P
+
+
+def define_figure_for(body, device_axis, a_name):
+    state_now = lax.psum(body, axis_name=device_axis)
+    return lax.psum(state_now, axis_name=a_name)
 
 
 def weight_grad(feats, cotan):
@@ -52,7 +57,7 @@
     )
     rpn_local = weight_grad(rpn_feats, rpn_cot)
     local_counts = jnp.stack([jnp.sum(roi_counts), jnp.sum(anchor_counts)]).astype(jnp.float32)
-    mask_sum, rpn_sum, totals = lax.psum((mask_local, rpn_local, local_counts), ("gx", "gy"))
+    mask_sum, rpn_sum, totals = define_figure_for((mask_local, rpn_local, local_counts), "gy", "gx")
     mask_grad = mask_sum / totals[0]
     rpn_grad = rpn_sum / totals[1]
     new_mask_weight, new_mask_moment = step_update(mask_weight, mask_moment, mask_grad)

time: 260 us -> 380 us (1.46)
  waiting for transfers between devices: 102 us -> 238 us
  blocking collectives: 42.4 us -> 25.8 us
    psum x1 -> x2, waiting for transfers between devices: 102 us -> 238 us  [the longest x1 172 us: define_figure_for(): state_now = lax.psum(body, axis_name=device_axis)]
    psum x1 -> x2, blocking collectives: 42.4 us -> 25.8 us  [the longest x1 19.3 us: define_figure_for(): state_now = lax.psum(body, axis_name=device_axis)]
  transfers between devices with their start and end apart: 1 -> 2, of which waited for: 1 -> 2; matrix products, arithmetic and copies ran while one was open for 1% -> 1% of each run, Pallas kernels for 0% -> 0%
where the time goes in v1:
time: 380 us; the launch traced here: 379 us
  waiting for transfers between devices  238 us (63%)
  local copies, waits for them, and re-layouts  54.6 us (14%)
  matrix products  30 us (8%)
  blocking collectives  25.8 us (7%)
  other arithmetic  15.6 us (4%)
  between operations  14.2 us (4%)
    psum x1, waiting for transfers between devices, define_figure_for(): state_now = lax.psum(body, axis_name=device_axis)  172 us
    psum x1, waiting for transfers between devices, define_figure_for(): return lax.psum(state_now, axis_name=a_name)  65.9 us
    dot_general x18, matrix products, weight_grad(): lax.dot_general(window, flat_cot, (((0,), (0,)), ((), ())), preferred_ele...  30 us
    slice x9, local copies, waits for them, and re-layouts, weight_grad(): padded[:, row_tap:row_tap + grid_rows, col_tap:col_tap + grid_cols, :]  22.6 us
    reshape x8, local copies, waits for them, and re-layouts, weight_grad(): window = padded[:, row_tap:row_tap + grid_rows, col_tap:col_tap + grid_co...  20.1 us
    psum x1, blocking collectives, define_figure_for(): state_now = lax.psum(body, axis_name=device_axis)  19.3 us
    sub x1, other arithmetic, step_update(): return (weight - 0.02 * fresh_moment, fresh_moment)  10.5 us
  transfers between devices with their start and end apart: 2, of which 2 were waited for; matrix products, arithmetic and copies ran while one was open for 1% of the time, Pallas kernels for 0%

profile of v1, /device:TPU:0, one launch (start us, length us, event | category | flops | bytes accessed | tf_op | source)
XLA Modules:
  0.0 378.6 jit_solution(16341040553515071347)
XLA Ops:
  7.2 0.0 copy-start
  7.2 0.0 all-reduce.7.cloned.1.call-start
  7.2 0.8 compare_convert_fusion
  8.1 1.6 broadcast_multiply_fusion
  9.7 1.6 copy.29
  11.3 3.7 reshape_reshape.3
  15.0 1.6 copy.81
  16.5 4.3 %pad_slice_fusion = (bf16[16,14,14,256]{3,0,2,1:T(8,128)(2,1)}, bf16[16,14,14,256]{3,0,2,1:T(8,128)(2,1)}, bf16[16,14,14,256]{3,0,2,1:T(8,128)(2,1)}, bf16[16,14...) fusion(bf16[16,14,14,256]{3,0,2,1:T(8,128)(2,1)S(1)} %bitcast.89), kind=kLoop, calls=%fused_computation.4 | loop fusion | bytes 14450688 | tf_op jit(solution)/shard_map/slice | solution.py:21
  20.8 1.8 copy.28
  22.7 3.6 reshape.70
  26.3 3.3 copy.30
  29.6 3.6 reshape.71
  33.2 3.3 copy.31
  36.5 3.6 reshape.72
  40.1 3.3 copy.32
  43.3 3.7 reshape.73
  47.0 3.4 convolution_dynamic-update-slice_fusion.7
  50.4 1.3 convolution_dynamic-update-slice_fusion.6
  51.8 0.1 copy-done.12
  51.8 1.3 convolution_dynamic-update-slice_fusion.5
  53.2 0.1 copy-done.13
  53.3 1.3 convolution_dynamic-update-slice_fusion.4
  54.6 0.1 copy-done.2
  54.7 1.5 fusion.25
  56.2 0.6 copy.35
  56.8 1.4 reshape.74
  58.2 2.0 copy.36
  60.2 1.4 reshape.75
  61.6 2.0 copy.37
  63.6 1.4 reshape.76
  65.0 2.0 copy.38
  67.1 1.4 reshape.77
  68.5 2.3 copy.39
  70.8 1.8 fusion.24
  72.6 2.1 fusion.22
  74.7 2.0 fusion.20
  76.7 1.3 fusion.18
  78.1 0.1 copy-done.3
  78.1 0.6 fusion.8
  78.8 1.3 fusion.16
  80.1 2.1 fusion.14
  82.2 2.3 fusion.12
  84.5 2.1 fusion.10
  86.6 1.3 convolution_dynamic-update-slice_fusion.3
  88.0 0.1 copy-done.4
  88.1 0.9 copy-done.8
  89.0 1.4 convolution_dynamic-update-slice_fusion.2
  90.3 0.1 copy-done.9
  90.4 1.4 convolution_dynamic-update-slice_fusion.1
  91.8 0.0 copy-done.10
  91.8 1.4 convolution_dynamic-update-slice_fusion
  93.2 0.0 all-reduce.7.cloned.1.call-update
  93.2 0.0 all-reduce.9.cloned.1.call-start
  93.2 172.3 %all-reduce.7.cloned.1.call-done = (f32[2304,256]{1,0:T(8,128)}, f32[2304,256]{1,0:T(8,128)}) async-done(((f32[2304,256]{1,0:T(8,128)}, f32[2304,256]{1,0:T(8,128)}), (f32[2304,256]{1,0:T(8,128)}, f32[2304,256]{1,0:T(8,128)})) %all-reduce.7.cloned.1.call-update) | async-done | bytes 4718608 | tf_op jit(solution)/shard_map/psum | solution.py:8
  265.6 0.0 all-reduce.9.cloned.1.call-update
  265.6 0.6 copy-done.14
  266.2 0.6 reduce_sum.18
  266.9 0.6 reduce_sum.19
  267.5 1.4 add_convert_fusion
  268.9 19.3 %psum.44 = f32[2]{0:T(128)S(1)} all-reduce(f32[2]{0:T(128)S(1)} %add_convert_fusion), channel_id=1, replica_groups=mesh['gx'=4,'gy'=8] {'gy'}, use_global_device_ids=true, to_apply=%region_4.5 | all-reduce | flops 2 | bytes 16 | tf_op jit(solution)/shard_map/psum | solution.py:8
  288.2 6.5 %psum.45 = f32[2]{0:T(128)S(1)} all-reduce(f32[2]{0:T(128)S(1)} %psum.44), channel_id=1, replica_groups=mesh['gx'=4,'gy'=8] {'gx'}, use_global_device_ids=true, to_apply=%region_5.6 | all-reduce | flops 2 | bytes 16 | tf_op jit(solution)/shard_map/psum | solution.py:9
  294.7 0.7 fusion.42
  295.3 65.9 %all-reduce.9.cloned.1.call-done = (f32[2304,256]{1,0:T(8,128)}, f32[2304,256]{1,0:T(8,128)}) async-done(((f32[2304,256]{1,0:T(8,128)}, f32[2304,256]{1,0:T(8,128)}), (f32[2304,256]{1,0:T(8,128)}, f32[2304,256]{1,0:T(8,128)})) %all-reduce.9.cloned.1.call-update) | async-done | bytes 4718608 | tf_op jit(solution)/shard_map/psum | solution.py:9
  361.2 10.5 %multiply_subtract_fusion = (f32[2304,256]{1,0:T(8,128)}, f32[2304,256]{1,0:T(8,128)}, f32[2304,256]{1,0:T(8,128)}, f32[2304,256]{1,0:T(8,128)}) fusion(f32[2304,256]{1,0:T(8,128)} %param.17, f32[2304,256]{1,0:T(8,128)} %get-tuple-element.7, f32[]{:T(128)} %bitcast.25, f32[2304,256]{1,0:T(8,128)} %param.19, f32[2304,256]{1,0:T(8,128)} %param.16, ...), kind=kLoop, calls=%fused_computation | loop fusion | flops 5898240 | bytes 23592968 | tf_op jit(solution)/shard_map/sub | solution.py:34
  (22 shorter events, 0.0 us)
Async XLA Ops:
  7.2 63.6 %copy-start = (bf16[2,48,32,256]{3,2,1,0:T(8,128)(2,1)S(1)}, bf16[2,48,32,256]{3,2,1,0:T(8,128)(2,1)}, u32[]{:S(2)}) copy-start(bf16[2,48,32,256]{3,2,1,0:T(8,128)(2,1)} %param.14) | copy-start | bytes 4718596
  7.2 258.4 %all-reduce.7.cloned.1.call-start = ((), (), s32[]{:S(2)}) async-start(), calls=%async_computation | async-start | bytes 9437184 | tf_op jit(solution)/shard_map/psum | solution.py:8
  47.0 3.4 copy-start.5
  47.0 3.4 copy-start.11
  50.4 1.4 copy-start.12
  51.8 1.4 copy-start.13
  53.2 1.4 copy-start.2
  54.7 1.5 copy-start.1
  76.7 1.4 copy-start.3
  84.5 2.1 copy-start.6
  84.5 2.1 copy-start.7
  86.6 1.5 copy-start.4
  86.6 2.4 copy-start.8
  89.0 1.4 copy-start.9
  90.4 1.4 copy-start.10
  93.2 268.0 %all-reduce.9.cloned.1.call-start = ((), (), s32[]{:S(2)}) async-start(), calls=%async_computation.1 | async-start | bytes 9437184 | tf_op jit(solution)/shard_map/psum | solution.py:9
  265.6 0.7 copy-start.14
  265.6 1.3 copy-start.15
Sparse Core Ops, SparseCore 0:
  93.3 172.2 all-reduce.6
  268.0 93.1 all-reduce.8
